TPU v7x, 32 devices: a whole 2x2x4 slice. The times are simulated.
32 devices in a mesh: sec: 8 (over y, x, core), pan: 4 (over z).
Axes of the slice: x: 2, y: 2, z: 4, core: 2. Of those that a mesh axis runs over, the one named last changes fastest.
Arguments:
- wave_state: bfloat16 [8, 512, 512], P('sec', 'pan'), may hold values from -6 to 6
- right_blocks: bfloat16 [8, 16, 512, 512], P('sec', None, None, 'pan'), may hold values from -0.25 to 0.25
- left_blocks: bfloat16 [576, 512, 512], P('sec', 'pan'), may hold values from -0.125 to 0.125
- coupling: bfloat16 [576], P('sec'), may hold values from -1 to 1
- channel_term: int32 [576], P('sec'), may hold values from 0 to 15
- channel_out: int32 [576], P('sec'), may hold values from 0 to 7, as said below
- sector_dims: int32 [8], P('sec'), may hold values from 128 to 512
Outputs:
- applied: float32 [8, 512, 512], P('sec', 'pan')
Inputs may be any that keep to these rules, and one draw needn't show every extreme that they name: `channel_out`: channel c ends in a sector at most two away from the sector c // 72 that it starts from.
All inputs are finite; a program needn't handle non-finite values.
Results may differ from a plain program's by a relative error of at most 0.0041.
Values may be sent and summed in bfloat16 or wider, within the bound.
A program may use at most 128 MiB of HBM per device.

v0:
```python
import jax
import jax.numpy as jnp
from jax import lax
from jax.sharding import PartitionSpec as P


def passed_along(value, axis, steps):
    count = lax.axis_size(axis)
    first, last = (max(0, -steps), min(count, count - steps))
    return lax.ppermute(value, axis, [(source, source + steps) for source in range(first, last)])


def on_device(
    wave_state, right_blocks, left_blocks, coupling, channel_term, channel_out, sector_dims
):
    panel_rows = wave_state.shape[1]
    block_width = wave_state.shape[2]
    term_count = right_blocks.shape[1]
    channels = left_blocks.shape[0]
    sector = lax.axis_index("sec")
    live_dim = sector_dims[0]
    whole_state = lax.all_gather(wave_state[0], "pan", axis=0, tiled=True)
    indices = lax.iota(jnp.int32, block_width)
    inside = (indices[:, None] < live_dim) & (indices[None, :] < live_dim)
    masked = jnp.where(inside, whole_state, jnp.zeros((), jnp.bfloat16))
    slot_ids = lax.iota(jnp.int32, 5)
    term_ids = lax.iota(jnp.int32, term_count)
    slot_index = channel_out - sector + 2
    chosen = (slot_index[None, None, :] == slot_ids[:, None, None]) & (
        channel_term[None, None, :] == term_ids[None, :, None]
    )
    weights = jnp.where(chosen, coupling[None, None, :], jnp.zeros((), jnp.bfloat16)).reshape(
        5 * term_count, channels
    )
    combined = jnp.dot(
        weights,
        left_blocks.reshape(channels, panel_rows * block_width),
        preferred_element_type=jnp.float32,
    )
    combined = combined.astype(jnp.bfloat16).reshape(5, term_count, panel_rows, block_width)
    right_full = lax.all_gather(right_blocks[0], "pan", axis=2, tiled=True)
    term_full = jnp.einsum(
        "ik,wkq->wiq", masked, right_full, preferred_element_type=jnp.float32
    ).astype(jnp.bfloat16)
    partial_value = jnp.einsum(
        "jwri,wiq->jrq", combined, term_full, preferred_element_type=jnp.float32
    )
    collected = partial_value[2][None]
    for offset in (-2, -1, 1, 2):
        collected = collected + passed_along(partial_value[offset + 2][None], "sec", offset)
    row_ids = lax.axis_index("pan") * panel_rows + lax.iota(jnp.int32, panel_rows)
    kept_mask = (row_ids[:, None] < live_dim) & (indices[None, :] < live_dim)
    return jnp.where(kept_mask[None], collected, jnp.zeros((), jnp.float32))


def solution(mesh):
    return jax.shard_map(
        on_device,
        mesh=mesh,
        in_specs=(
            P("sec", "pan", None),
            P("sec", None, None, "pan"),
            P("sec", "pan", None),
            P("sec"),
            P("sec"),
            P("sec"),
            P("sec"),
        ),
        out_specs=P("sec", "pan", None),
        check_vma=False,
    )
```

profile of v0, /device:TPU:4, one launch (start us, length us, event | category | flops | bytes accessed | tf_op | source)
XLA Modules:
  0.0 216.9 jit_solution(9259897033509172264)
XLA Ops:
  6.5 0.0 all-gather.4.cloned.1.call-start
  6.5 0.7 all-gather.4.cloned.1.call-update
  7.9 0.0 copy-start.4
  7.9 0.0 copy-start.2
  7.9 0.0 copy-start.3
  7.9 13.8 %copy.9 = bf16[9,8,128,512]{3,1,2,0:T(8,128)(2,1)} copy(bf16[9,8,128,512]{3,2,1,0:T(8,128)(2,1)} %bitcast.41) | data formatting | bytes 18874368
  21.7 0.0 copy-done.4
  21.7 0.0 copy-done.2
  21.7 0.0 copy-done.3
  21.8 10.6 %convolution_convert_fusion = bf16[80,65536]{1,0:T(8,128)(2,1)} fusion(bf16[80,72]{1,0:T(8,128)(2,1)S(1)} %bitcast.42, bf16[72,65536]{1,0:T(8,128)(2,1)} %bitcast.39), kind=kOutput, calls=%fused_computation | convolution fusion | flops 760217600 | bytes 19934464 | tf_op jit(solution)/shard_map/dot_general | solution.py:35
  32.3 0.0 copy-start.1
  32.3 12.4 %copy.10 = bf16[10,8,128,512]{3,2,1,0:T(8,128)(2,1)} copy(bf16[10,8,128,512]{3,1,2,0:T(8,128)(2,1)} %bitcast.38) | data formatting | bytes 20971520
  44.7 0.0 copy-done.1
  44.7 36.9 %all-gather = bf16[1,512,512]{2,1,0:T(8,128)(2,1)S(1)} all-gather(bf16[1,128,512]{2,1,0:T(8,128)(2,1)S(1)} %copy-done.1), channel_id=2, replica_groups=mesh['sec'=8,'pan'=4] {'pan'}, dimensions={1}, use_global_device_ids=true | all-gather | bytes 655360 | tf_op jit(solution)/shard_map/all_gather | solution.py:22
  81.6 86.0 %all-gather.4.cloned.1.call-done = bf16[1,16,512,512]{3,2,1,0:T(8,128)(2,1)} async-done(((bf16[1,16,512,128]{3,2,1,0:T(8,128)(2,1)}), bf16[1,16,512,512]{3,2,1,0:T(8,128)(2,1)}) %all-gather.4.cloned.1.call-update) | async-done | bytes 8388624 | tf_op jit(solution)/shard_map/all_gather | solution.py:41
  167.7 0.0 copy-start
  167.7 10.4 %fusion.3 = bf16[512,16,512]{2,0,1:T(8,128)(2,1)} fusion(bf16[1,16,512,512]{3,2,1,0:T(8,128)(2,1)} %all-gather.4.cloned.1.call-done, bf16[1,512,512]{2,1,0:T(8,128)(2,1)S(1)} %all-gather, pred[512]{0:T(512)(128)(4,1)S(1)} %iota_compare_fusion.2), kind=kOutput, calls=%fused_computation.4 | convolution fusion | flops 4295491584 | bytes 17302016 | tf_op jit(solution)/shard_map/ik,wkq->wiq/dot_general | solution.py:42
  178.1 0.0 copy-done
  178.1 9.5 %fusion.6 = f32[5,128,512]{2,1,0:T(8,128)S(1)} fusion(bf16[512,16,512]{2,0,1:T(8,128)(2,1)} %fusion.3, bf16[5,16,128,512]{3,2,1,0:T(8,128)(2,1)S(1)} %bitcast.40), kind=kOutput, calls=%fused_computation.7 | convolution fusion | flops 5368709120 | bytes 20185088 | tf_op jit(solution)/shard_map/jwri,wiq->jrq/dot_general | solution.py:45
  187.6 0.1 fusion.22
  187.7 3.4 %collective-permute-start = (f32[1,128,512]{2,1,0:T(8,128)S(1)}, f32[1,128,512]{2,1,0:T(8,128)S(1)}, u32[]{:S(2)}, u32[]{:S(2)}) collective-permute-start(f32[1,128,512]{2,1,0:T(8,128)S(1)} %get-tuple-element.5), channel_id=1, source_target_pairs={{8,0},{12,4},{16,8},{20,12},{24,16},{28,20},{9,1},{13,5},{17,9},{2... | collective-permute-start | bytes 786440 | tf_op jit(solution)/shard_map/ppermute | solution.py:10
  191.0 2.5 %collective-permute-start.3 = (f32[1,128,512]{2,1,0:T(8,128)S(1)}, f32[1,128,512]{2,1,0:T(8,128)S(1)}, u32[]{:S(2)}, u32[]{:S(2)}) collective-permute-start(f32[1,128,512]{2,1,0:T(8,128)S(1)} %get-tuple-element.6), channel_id=1, source_target_pairs={{0,8},{4,12},{8,16},{12,20},{16,24},{20,28},{1,9},{5,13},{9,17},{1... | collective-permute-start | bytes 786440 | tf_op jit(solution)/shard_map/ppermute | solution.py:10
  193.5 1.9 collective-permute-start.2
  195.5 4.5 %collective-permute-start.1 = (f32[1,128,512]{2,1,0:T(8,128)S(1)}, f32[1,128,512]{2,1,0:T(8,128)S(1)}, u32[]{:S(2)}, u32[]{:S(2)}) collective-permute-start(f32[1,128,512]{2,1,0:T(8,128)S(1)} %get-tuple-element.8), channel_id=1, source_target_pairs={{4,0},{8,4},{12,8},{16,12},{20,16},{24,20},{28,24},{5,1},{9,5},{13... | collective-permute-start | bytes 786440 | tf_op jit(solution)/shard_map/ppermute | solution.py:10
  200.0 0.0 collective-permute-done
  200.0 5.8 %collective-permute-done.3 = f32[1,128,512]{2,1,0:T(8,128)S(1)} collective-permute-done((f32[1,128,512]{2,1,0:T(8,128)S(1)}, f32[1,128,512]{2,1,0:T(8,128)S(1)}, u32[]{:S(2)}, u32[]{:S(2)}) %collective-permute-start.3) | collective-permute-done | bytes 262176 | tf_op jit(solution)/shard_map/ppermute | solution.py:10
  205.8 3.4 %collective-permute-done.2 = f32[1,128,512]{2,1,0:T(8,128)S(1)} collective-permute-done((f32[1,128,512]{2,1,0:T(8,128)S(1)}, f32[1,128,512]{2,1,0:T(8,128)S(1)}, u32[]{:S(2)}, u32[]{:S(2)}) %collective-permute-start.2) | collective-permute-done | bytes 262176 | tf_op jit(solution)/shard_map/ppermute | solution.py:10
  209.2 0.0 collective-permute-done.1
  209.2 0.8 fusion.19
  (6 shorter events, 0.0 us)
Async XLA Ops:
  6.5 161.1 %all-gather.4.cloned.1.call-start = ((), (), s32[]{:S(2)}) async-start(), calls=%async_computation | async-start | bytes 10485760 | tf_op jit(solution)/shard_map/all_gather | solution.py:41
  7.9 13.8 %copy-start.4 = (s32[72]{0:T(128)S(1)}, s32[72]{0:T(128)}, u32[]{:S(2)}) copy-start(s32[72]{0:T(128)} %param.12) | copy-start | bytes 868
  7.9 13.8 %copy-start.2 = (s32[72]{0:T(128)S(1)}, s32[72]{0:T(128)}, u32[]{:S(2)}) copy-start(s32[72]{0:T(128)} %param.11) | copy-start | bytes 868
  7.9 13.8 %copy-start.3 = (bf16[72]{0:T(256)(128)(2,1)S(1)}, bf16[72]{0:T(256)(128)(2,1)}, u32[]{:S(2)}) copy-start(bf16[72]{0:T(256)(128)(2,1)} %param.10) | copy-start | bytes 436
  32.3 12.4 %copy-start.1 = (bf16[1,128,512]{2,1,0:T(8,128)(2,1)S(1)}, bf16[1,128,512]{2,1,0:T(8,128)(2,1)}, u32[]{:S(2)}) copy-start(bf16[1,128,512]{2,1,0:T(8,128)(2,1)} %param.7) | copy-start | bytes 393220
  167.7 10.4 %copy-start = (bf16[10,8,128,512]{3,2,1,0:T(8,128)(2,1)S(1)}, bf16[10,8,128,512]{3,2,1,0:T(8,128)(2,1)}, u32[]{:S(2)}) copy-start(bf16[10,8,128,512]{3,2,1,0:T(8,128)(2,1)} %copy.10) | copy-start | bytes 31457284
  187.7 12.4 %collective-permute-start = (f32[1,128,512]{2,1,0:T(8,128)S(1)}, f32[1,128,512]{2,1,0:T(8,128)S(1)}, u32[]{:S(2)}, u32[]{:S(2)}) collective-permute-start(f32[1,128,512]{2,1,0:T(8,128)S(1)} %get-tuple-element.5), channel_id=1, source_target_pairs={{8,0},{12,4},{16,8},{20,12},{24,16},{28,20},{9,1},{13,5},{17,9},{2... | collective-permute-start | bytes 786440 | tf_op jit(solution)/shard_map/ppermute | solution.py:10
  191.0 14.8 %collective-permute-start.3 = (f32[1,128,512]{2,1,0:T(8,128)S(1)}, f32[1,128,512]{2,1,0:T(8,128)S(1)}, u32[]{:S(2)}, u32[]{:S(2)}) collective-permute-start(f32[1,128,512]{2,1,0:T(8,128)S(1)} %get-tuple-element.6), channel_id=1, source_target_pairs={{0,8},{4,12},{8,16},{12,20},{16,24},{20,28},{1,9},{5,13},{9,17},{1... | collective-permute-start | bytes 786440 | tf_op jit(solution)/shard_map/ppermute | solution.py:10
  193.5 15.7 %collective-permute-start.2 = (f32[1,128,512]{2,1,0:T(8,128)S(1)}, f32[1,128,512]{2,1,0:T(8,128)S(1)}, u32[]{:S(2)}, u32[]{:S(2)}) collective-permute-start(f32[1,128,512]{2,1,0:T(8,128)S(1)} %get-tuple-element.7), channel_id=1, source_target_pairs={{0,4},{4,8},{8,12},{12,16},{16,20},{20,24},{24,28},{1,5},{5,9},{9,... | collective-permute-start | bytes 786440 | tf_op jit(solution)/shard_map/ppermute | solution.py:10
  195.5 13.8 %collective-permute-start.1 = (f32[1,128,512]{2,1,0:T(8,128)S(1)}, f32[1,128,512]{2,1,0:T(8,128)S(1)}, u32[]{:S(2)}, u32[]{:S(2)}) collective-permute-start(f32[1,128,512]{2,1,0:T(8,128)S(1)} %get-tuple-element.8), channel_id=1, source_target_pairs={{4,0},{8,4},{12,8},{16,12},{20,16},{24,20},{28,24},{5,1},{9,5},{13... | collective-permute-start | bytes 786440 | tf_op jit(solution)/shard_map/ppermute | solution.py:10
Sparse Core Ops, SparseCore 0:
  8.9 158.7 all-gather.3
where the time goes:
time: 219 us; the launch traced here: 217 us
  waiting for transfers between devices  95.9 us (44%)
  blocking collectives  36.9 us (17%)
  matrix products  30.5 us (14%)
  local copies, waits for them, and re-layouts  26.2 us (12%)
  between operations  14.2 us (6%)
  starting transfers between devices  12.3 us (6%)
    all_gather x1, waiting for transfers between devices, on_device(): right_full = lax.all_gather(right_blocks[0], 'pan', axis=2, tiled=True)  86 us
    all_gather x1, blocking collectives, on_device(): whole_state = lax.all_gather(wave_state[0], 'pan', axis=0, tiled=True)  36.9 us
    unnamed x12, local copies, waits for them, and re-layouts  26.2 us
    ppermute x4, starting transfers between devices, passed_along(): lax.ppermute(value, axis, [(source, source + steps) for source in range(f...  12.3 us
    dot_general x1, matrix products, on_device(): jnp.dot(weights, left_blocks.reshape(channels, panel_rows * block_width),...  10.6 us
    dot_general x1, matrix products, on_device(): jnp.einsum('ik,wkq->wiq', masked, right_full, preferred_element_type=jnp....  10.4 us
    dot_general x1, matrix products, on_device(): jnp.einsum('jwri,wiq->jrq', combined, term_full, preferred_element_type=j...  9.49 us
    ppermute x4, waiting for transfers between devices, passed_along(): lax.ppermute(value, axis, [(source, source + steps) for source in range(f...  9.18 us
  transfers between devices with their start and end apart: 5, of which 3 were waited for; matrix products, arithmetic and copies ran while one was open for 17% of the time, Pallas kernels for 0%

commit v1 on v0

v1 whole, which is shorter than its diff:
```python
import functools

import jax
import jax.numpy as jnp
from jax import lax
from jax.experimental import pallas as pl
from jax.experimental.pallas import tpu as pltpu
from jax.sharding import PartitionSpec as P

OFFSETS = (-2, -1, 1, 2)
F32 = jnp.float32
BF16 = jnp.bfloat16


def combine_kernel(cell_ref, coef_ref, left_ref, out_ref, acc_ref):
    acc_ref[...] = jnp.zeros_like(acc_ref)

    @pl.loop(0, left_ref.shape[0])
    def _(channel):
        cell = cell_ref[channel]
        acc_ref[cell] += left_ref[channel].astype(F32) * coef_ref[channel]

    @pl.loop(0, out_ref.shape[0])
    def _(cell):
        out_ref[cell] = acc_ref[cell].astype(BF16)


def combine(cells, coefs, left_blocks, cell_count):
    channels, rows, width = left_blocks.shape
    step = min(rows, 32)
    return pl.pallas_call(
        combine_kernel,
        grid=(rows // step,),
        in_specs=[
            pl.BlockSpec(memory_space=pltpu.SMEM),
            pl.BlockSpec(memory_space=pltpu.SMEM),
            pl.BlockSpec((channels, step, width), lambda i: (0, i, 0)),
        ],
        out_specs=pl.BlockSpec((cell_count, step, width), lambda i: (0, i, 0)),
        out_shape=jax.ShapeDtypeStruct((cell_count, rows, width), BF16),
        scratch_shapes=[pltpu.VMEM((cell_count, step, width), F32)],
        compiler_params=pltpu.CompilerParams(vmem_limit_bytes=48 * 2**20),
    )(cells, coefs, left_blocks)


def line_kernel(
    sectors, moved, dims_ref, state_ref, right_ref, comb_ref, out_ref,
    state_all, masked, gathered, comb, comb_end, acc, acc_end,
    stage, landed, stage_end, landed_end, back, back_landed,
    local_sems, state_send, state_recv, own_send, relay_send, right_recv,
    end_send, end_recv, part_send, part_recv, part_end_send, part_end_recv, back_sems,
):
    terms, width, cols = right_ref.shape
    rows = state_ref.shape[0]
    me = lax.axis_index("pan")
    sector = lax.axis_index("sec")
    is_mid = (me == 1) | (me == 2)
    is_end = jnp.logical_not(is_mid)
    near_end = jnp.where(me <= 1, 0, 3)
    other_mid = jnp.where(me <= 1, 2, 1)
    far_end = 3 - near_end
    near_mid = jnp.where(me <= 1, 1, 2)

    def remote(src, dst, send, recv, where, axis="pan"):
        return pltpu.make_async_remote_copy(
            src_ref=src, dst_ref=dst, send_sem=send, recv_sem=recv,
            device_id={axis: where}, device_id_type=pl.DeviceIdType.MESH,
        )

    def state_copy(shift):
        where = lax.rem(me + shift, 4)
        spot = state_all.at[me]
        return remote(state_ref, spot, state_send.at[shift], state_recv.at[me], where)

    def state_wait(owner):
        remote(state_ref, state_all.at[owner], state_send.at[0], state_recv.at[owner], me).wait_recv()

    def own_copy(way, term, where):
        return remote(
            right_ref.at[term], gathered.at[me, term],
            own_send.at[way, term], right_recv.at[me, term], where,
        )

    def relay_copy(way, owner, term, where):
        block = gathered.at[owner, term]
        return remote(block, block, relay_send.at[way, term], right_recv.at[owner, term], where)

    def end_copy(term):
        return remote(comb_ref.at[term], comb_end.at[term], end_send.at[term], end_recv.at[term], near_mid)

    def arrived(owner, term):
        block = gathered.at[owner, term]
        remote(block, block, relay_send.at[0, term], right_recv.at[owner, term], me).wait_recv()

    def part_copy(index, owner):
        return remote(
            stage.at[index, owner], landed.at[index, owner],
            part_send.at[index, owner], part_recv.at[index, owner], sector + OFFSETS[index], "sec",
        )

    def part_end_copy(index):
        return remote(
            stage_end.at[index], landed_end.at[index],
            part_end_send.at[index], part_end_recv.at[index], sector + OFFSETS[index], "sec",
        )

    def goes(index):
        target = sector + OFFSETS[index]
        return (target >= 0) & (target < sectors)

    def comes(index):
        source = sector - OFFSETS[index]
        return (source >= 0) & (source < sectors)

    for shift in (1, 2, 3):
        state_copy(shift).start()

    @pl.when(is_mid)
    def _():
        @pl.loop(0, terms)
        def _(term):
            own_copy(0, term, other_mid).start()

            @pl.when(term >= moved)
            def _():
                own_copy(1, term, near_end).start()

    @pl.when(is_end)
    def _():
        @pl.loop(0, terms)
        def _(term):
            own_copy(0, term, near_mid).start()

        @pl.loop(0, moved)
        def _(term):
            end_copy(term).start()

    copies = [
        pltpu.make_async_copy(state_ref, state_all.at[me], local_sems.at[0]),
        pltpu.make_async_copy(right_ref, gathered.at[me], local_sems.at[1]),
        pltpu.make_async_copy(comb_ref, comb, local_sems.at[2]),
    ]
    for copy in copies:
        copy.start()
    acc[...] = jnp.zeros_like(acc)
    acc_end[...] = jnp.zeros_like(acc_end)
    for copy in copies:
        copy.wait()
    for shift in (1, 2, 3):
        state_wait(lax.rem(me + shift, 4))
    live = dims_ref[0]
    inside_col = lax.broadcasted_iota(jnp.int32, (rows, width), 1) < live
    for owner in range(4):
        row = lax.broadcasted_iota(jnp.int32, (rows, width), 0) + owner * rows
        masked[owner * rows:(owner + 1) * rows, :] = jnp.where(
            inside_col & (row < live), state_all[owner].astype(F32), 0.0
        ).astype(BF16)

    def multiply(owner, term, left, total):
        block = jnp.dot(masked[...], gathered[owner, term], preferred_element_type=F32).astype(BF16)
        total[owner] += jnp.dot(left[term], block, preferred_element_type=F32)

    def send_parts(owner):
        for index in range(4):
            slot = OFFSETS[index] + 2

            @pl.when(goes(index))
            def _():
                stage[index, owner] = acc[owner, slot * rows:(slot + 1) * rows, :].astype(BF16)
                part_copy(index, owner).start()

    @pl.when(is_mid)
    def _():
        @pl.loop(0, terms)
        def _(term):
            arrived(other_mid, term)

            @pl.when(term >= moved)
            def _():
                relay_copy(0, other_mid, term, near_end).start()

            arrived(near_end, term)
            relay_copy(1, near_end, term, other_mid).start()

            @pl.loop(0, 3)
            def _(which):
                owner = jnp.where(which == 0, me, jnp.where(which == 1, other_mid, near_end))
                multiply(owner, term, comb, acc)

        @pl.loop(0, 3)
        def _(which):
            send_parts(jnp.where(which == 0, me, jnp.where(which == 1, other_mid, near_end)))

        @pl.loop(0, terms)
        def _(term):
            arrived(far_end, term)

            @pl.when(term >= moved)
            def _():
                relay_copy(2, far_end, term, near_end).start()

            multiply(far_end, term, comb, acc)

        send_parts(far_end)

        @pl.loop(0, moved)
        def _(term):
            remote(comb_ref.at[term], comb_end.at[term], end_send.at[term], end_recv.at[term], me).wait_recv()

            @pl.loop(0, 4)
            def _(owner):
                multiply(owner, term, comb_end, acc_end)

        for index in range(4):
            slot = OFFSETS[index] + 2

            @pl.when(goes(index))
            def _():
                stage_end[index] = acc_end[:, slot * rows:(slot + 1) * rows, :].astype(BF16)
                part_end_copy(index).start()

        for index in range(4):
            @pl.when(comes(index))
            def _():
                part_end_copy(index).wait_recv()
                acc_end[:, 2 * rows:3 * rows, :] += landed_end[index].astype(F32)

        back[...] = acc_end[:, 2 * rows:3 * rows, :].astype(BF16)
        remote(back, back_landed, back_sems.at[0], back_sems.at[1], near_end).start()

    @pl.when(is_end)
    def _():
        turn = jnp.where(me == 0, 1, -1)

        @pl.loop(0, 4)
        def _(rank):
            owner = me + turn * rank

            @pl.loop(moved, terms)
            def _(term):
                @pl.when(rank > 0)
                def _():
                    arrived(owner, term)

                multiply(owner, term, comb, acc)

            send_parts(owner)

    for index in range(4):
        @pl.when(comes(index))
        def _():
            @pl.loop(0, 4)
            def _(owner):
                part_copy(index, owner).wait_recv()
                acc[owner, 2 * rows:3 * rows, :] += landed[index, owner].astype(F32)

    @pl.when(is_end)
    def _():
        remote(back, back_landed, back_sems.at[0], back_sems.at[1], me).wait_recv()
        acc[:, 2 * rows:3 * rows, :] += back_landed[...].astype(F32)

    for owner in range(4):
        out_ref[:, owner * cols:(owner + 1) * cols] = acc[owner, 2 * rows:3 * rows, :]

    for shift in (1, 2, 3):
        state_copy(shift).wait_send()
    for index in range(4):
        @pl.when(goes(index))
        def _():
            @pl.loop(0, 4)
            def _(owner):
                part_copy(index, owner).wait_send()

            @pl.when(is_mid)
            def _():
                part_end_copy(index).wait_send()

    @pl.when(is_mid)
    def _():
        @pl.loop(0, terms)
        def _(term):
            own_copy(0, term, other_mid).wait_send()
            relay_copy(1, near_end, term, other_mid).wait_send()

            @pl.when(term >= moved)
            def _():
                own_copy(1, term, near_end).wait_send()
                relay_copy(0, other_mid, term, near_end).wait_send()
                relay_copy(2, far_end, term, near_end).wait_send()

        remote(back, back_landed, back_sems.at[0], back_sems.at[1], near_end).wait_send()

    @pl.when(is_end)
    def _():
        @pl.loop(0, terms)
        def _(term):
            own_copy(0, term, near_mid).wait_send()

        @pl.loop(0, moved)
        def _(term):
            end_copy(term).wait_send()


def line_apply(sectors, dims, state, right, combined):
    terms, width, cols = right.shape
    rows = state.shape[0]
    moved = max(1, (terms * 3) // 16)
    tall = combined.shape[1]
    dma = pltpu.SemaphoreType.DMA
    any_space = pl.BlockSpec(memory_space=pl.ANY)
    return pl.pallas_call(
        functools.partial(line_kernel, sectors, moved),
        out_shape=jax.ShapeDtypeStruct((rows, width), F32),
        in_specs=[pl.BlockSpec(memory_space=pltpu.SMEM), any_space, any_space, any_space],
        out_specs=pl.BlockSpec(memory_space=pltpu.VMEM),
        scratch_shapes=[
            pltpu.VMEM((4, rows, width), BF16),
            pltpu.VMEM((width, width), BF16),
            pltpu.VMEM((4, terms, width, cols), BF16),
            pltpu.VMEM((terms, tall, width), BF16),
            pltpu.VMEM((moved, tall, width), BF16),
            pltpu.VMEM((4, tall, cols), F32),
            pltpu.VMEM((4, tall, cols), F32),
            pltpu.VMEM((4, 4, rows, cols), BF16),
            pltpu.VMEM((4, 4, rows, cols), BF16),
            pltpu.VMEM((4, 4, rows, cols), BF16),
            pltpu.VMEM((4, 4, rows, cols), BF16),
            pltpu.VMEM((4, rows, cols), BF16),
            pltpu.VMEM((4, rows, cols), BF16),
            dma((3,)), dma((4,)), dma((4,)),
            dma((2, terms)), dma((3, terms)), dma((4, terms)),
            dma((moved,)), dma((moved,)),
            dma((4, 4)), dma((4, 4)), dma((4,)), dma((4,)), dma((2,)),
        ],
        compiler_params=pltpu.CompilerParams(
            has_side_effects=True, vmem_limit_bytes=56 * 2**20
        ),
    )(dims, state, right, combined)


def passed_along(value, axis, steps):
    count = lax.axis_size(axis)
    first, last = (max(0, -steps), min(count, count - steps))
    return lax.ppermute(value, axis, [(source, source + steps) for source in range(first, last)])


def gathered_apply(sector, live_dim, wave, right, combined, rows, slots):
    width = wave.shape[1]
    terms = right.shape[0]
    whole_state = lax.all_gather(wave, "pan", axis=0, tiled=True)
    indices = lax.iota(jnp.int32, width)
    inside = (indices[:, None] < live_dim) & (indices[None, :] < live_dim)
    masked = jnp.where(inside, whole_state, jnp.zeros((), BF16))
    right_full = lax.all_gather(right, "pan", axis=2, tiled=True)
    term_full = jnp.einsum("ik,wkq->wiq", masked, right_full, preferred_element_type=F32).astype(BF16)
    parts = jnp.einsum(
        "wjri,wiq->jrq", combined.reshape(terms, slots, rows, width), term_full,
        preferred_element_type=F32,
    )
    collected = parts[2]
    for offset in OFFSETS:
        collected = collected + passed_along(parts[offset + 2], "sec", offset)
    return collected


def on_device(
    wave_state, right_blocks, left_blocks, coupling, channel_term, channel_out, sector_dims
):
    rows, width = wave_state.shape[1:]
    terms = right_blocks.shape[1]
    slots = 5
    sector = lax.axis_index("sec")
    live_dim = sector_dims[0]
    cells = channel_term * slots + channel_out - sector + 2
    combined = combine(cells, coupling.astype(F32), left_blocks, terms * slots)
    if lax.axis_size("pan") == 4 and right_blocks.shape[3] % 128 == 0:
        collected = line_apply(
            lax.axis_size("sec"), sector_dims, wave_state[0], right_blocks[0],
            combined.reshape(terms, slots * rows, width),
        )
    else:
        collected = gathered_apply(
            sector, live_dim, wave_state[0], right_blocks[0], combined, rows, slots
        )
    indices = lax.iota(jnp.int32, width)
    row_ids = lax.axis_index("pan") * rows + lax.iota(jnp.int32, rows)
    kept_mask = (row_ids[:, None] < live_dim) & (indices[None, :] < live_dim)
    return jnp.where(kept_mask, collected, jnp.zeros((), F32))[None]


def solution(mesh):
    return jax.shard_map(
        on_device,
        mesh=mesh,
        in_specs=(
            P("sec", "pan", None),
            P("sec", None, None, "pan"),
            P("sec", "pan", None),
            P("sec"),
            P("sec"),
            P("sec"),
            P("sec"),
        ),
        out_specs=P("sec", "pan", None),
        check_vma=False,
    )
```

time: 219 us -> 153 us (0.70)
  Pallas kernels: 0 us -> 149 us
  waiting for transfers between devices: 95.9 us -> 0 us
  blocking collectives: 36.9 us -> 0 us
  matrix products: 30.5 us -> 0 us
  local copies, waits for them, and re-layouts: 26.2 us -> 0 us
  between operations: 14.2 us -> 0.68 us
  starting transfers between devices: 12.3 us -> 0 us
  other arithmetic: 0.84 us -> 3.1 us
    pallas_call x0 -> x2, Pallas kernels: none -> 149 us  [the longest x1 138 us: line_apply(): pl.pallas_call(functools.partial(line_kernel, sectors, moved), out_shape=...]
    all_gather x1 -> x0, waiting for transfers between devices: 86 us -> none  [on_device(): right_full = lax.all_gather(right_blocks[0], 'pan', axis=2, tiled=True)]
    all_gather x1 -> x0, blocking collectives: 36.9 us -> none  [on_device(): whole_state = lax.all_gather(wave_state[0], 'pan', axis=0, tiled=True)]
    dot_general x3 -> x0, matrix products: 30.5 us -> none  [the longest x1 10.6 us: on_device(): jnp.dot(weights, left_blocks.reshape(channels, panel_rows * block_width),...]
    unnamed x12 -> x0, local copies, waits for them, and re-layouts: 26.2 us -> none
    ppermute x4 -> x0, starting transfers between devices: 12.3 us -> none  [passed_along(): lax.ppermute(value, axis, [(source, source + steps) for source in range(f...]
    ppermute x4 -> x0, waiting for transfers between devices: 9.18 us -> none  [passed_along(): lax.ppermute(value, axis, [(source, source + steps) for source in range(f...]
  transfers between devices with their start and end apart: 5 -> 0, of which waited for: 3 -> 0; matrix products, arithmetic and copies ran while one was open for 17% -> 0% of each run, Pallas kernels for 0% -> 0%
where the time goes in v1:
time: 153 us
  Pallas kernels  149 us (97%)
  other arithmetic  3.1 us (2%)
    pallas_call x1, Pallas kernels, line_apply(): pl.pallas_call(functools.partial(line_kernel, sectors, moved), out_shape=...  138 us
    pallas_call x1, Pallas kernels, combine(): pl.pallas_call(combine_kernel, grid=(rows // step,), in_specs=[pl.BlockSp...  11.5 us

profile of v1, /device:TPU:4, one launch (start us, length us, event | category | flops | bytes accessed | tf_op | source)
XLA Modules:
  0.0 152.8 jit_solution(6179714271755222422)
XLA Ops:
  0.7 0.7 subtract_add_fusion.cell_ref
  1.3 0.7 convert_element_type.3.coef_ref
  2.0 11.5 %shard_map.73 = bf16[80,128,512]{2,1,0:T(8,128)(2,1)} custom-call(s32[72]{0:T(128)S(1)} %subtract_add_fusion.cell_ref, f32[72]{0:T(128)S(1)} %convert_element_type.3.coef_ref, bf16[72,128,512]{2,1,0:T(8,128)(2,1)} %left_ref.1), custom_call_target="tpu_custom_call" | custom-call | tf_op jit(solution)/shard_map/pallas_call | solution.py:31
  13.5 137.5 %shard_map.74 = f32[128,512]{1,0:T(8,128)} custom-call(s32[1]{0:T(128)} %copy.8.dims_ref, bf16[128,512]{1,0:T(8,128)(2,1)} %bitcast.10, bf16[16,512,128]{2,1,0:T(8,128)(2,1)} %bitcast.9, bf16[16,640,512]{2,1,0:T(8,128)(2,1)} %bitcast.8), custom_call_target="tpu_custom_call" | custom-call | tf_op jit(solution)/shard_map/pallas_call | solution.py:311
  151.0 1.8 %select_bitcast_fusion = f32[1,128,512]{2,1,0:T(8,128)} fusion(f32[128,512]{1,0:T(8,128)} %shard_map.74, pred[512]{0:T(512)(128)(4,1)S(1)} %iota_compare_fusion, pred[128]{0:T(512)(128)(4,1)S(1)} %add_compare_fusion), kind=kLoop, calls=%fused_computation | loop fusion | flops 131072 | bytes 524928 | tf_op jit(solution)/shard_map/broadcast_in_dim | solution.py:388
  (2 shorter events, 0.0 us)

commit v2 on v1

--- a/solution.py
+++ b/solution.py
@@ -40,11 +40,15 @@
         out_shape=jax.ShapeDtypeStruct((cell_count, rows, width), BF16),
         scratch_shapes=[pltpu.VMEM((cell_count, step, width), F32)],
         compiler_params=pltpu.CompilerParams(vmem_limit_bytes=48 * 2**20),
+        cost_estimate=pl.CostEstimate(
+            flops=2 * left_blocks.size, transcendentals=0,
+            bytes_accessed=10 * (left_blocks.size + cell_count * rows * width),
+        ),
     )(cells, coefs, left_blocks)
 
 
 def line_kernel(
-    sectors, moved, dims_ref, state_ref, right_ref, comb_ref, out_ref,
+    sectors, moved, early, dims_ref, state_ref, right_ref, below_ref, above_ref, comb_ref, out_ref,
     state_all, masked, gathered, comb, comb_end, acc, acc_end,
     stage, landed, stage_end, landed_end, back, back_landed,
     local_sems, state_send, state_recv, own_send, relay_send, right_recv,
@@ -112,24 +116,27 @@
         source = sector - OFFSETS[index]
         return (source >= 0) & (source < sectors)
 
+    def term_of(step):
+        return lax.rem(step + moved, terms)
+
     for shift in (1, 2, 3):
         state_copy(shift).start()
 
     @pl.when(is_mid)
     def _():
-        @pl.loop(0, terms)
-        def _(term):
-            own_copy(0, term, other_mid).start()
-
-            @pl.when(term >= moved)
-            def _():
-                own_copy(1, term, near_end).start()
+        @pl.loop(early, terms)
+        def _(step):
+            own_copy(0, term_of(step), other_mid).start()
+
+            @pl.when(step < terms - moved)
+            def _():
+                own_copy(1, term_of(step), near_end).start()
 
     @pl.when(is_end)
     def _():
-        @pl.loop(0, terms)
-        def _(term):
-            own_copy(0, term, near_mid).start()
+        @pl.loop(early, terms)
+        def _(step):
+            own_copy(0, term_of(step), near_mid).start()
 
         @pl.loop(0, moved)
         def _(term):
@@ -140,12 +147,37 @@
         pltpu.make_async_copy(right_ref, gathered.at[me], local_sems.at[1]),
         pltpu.make_async_copy(comb_ref, comb, local_sems.at[2]),
     ]
+    spread = pl.ds(moved, early)
+    below = pltpu.make_async_copy(
+        below_ref, gathered.at[jnp.maximum(me - 1, 0), spread], local_sems.at[3]
+    )
+    above = pltpu.make_async_copy(
+        above_ref, gathered.at[jnp.minimum(me + 1, 3), spread], local_sems.at[4]
+    )
+
+    @pl.when(me > 0)
+    def _():
+        below.start()
+
+    @pl.when(me < 3)
+    def _():
+        above.start()
+
     for copy in copies:
         copy.start()
     acc[...] = jnp.zeros_like(acc)
     acc_end[...] = jnp.zeros_like(acc_end)
     for copy in copies:
         copy.wait()
+
+    @pl.when(me > 0)
+    def _():
+        below.wait()
+
+    @pl.when(me < 3)
+    def _():
+        above.wait()
+
     for shift in (1, 2, 3):
         state_wait(lax.rem(me + shift, 4))
     live = dims_ref[0]
@@ -172,14 +204,21 @@
     @pl.when(is_mid)
     def _():
         @pl.loop(0, terms)
-        def _(term):
-            arrived(other_mid, term)
-
-            @pl.when(term >= moved)
+        def _(step):
+            term = term_of(step)
+
+            @pl.when(step >= early)
+            def _():
+                arrived(other_mid, term)
+
+            @pl.when(step < terms - moved)
             def _():
                 relay_copy(0, other_mid, term, near_end).start()
 
-            arrived(near_end, term)
+            @pl.when(step >= early)
+            def _():
+                arrived(near_end, term)
+
             relay_copy(1, near_end, term, other_mid).start()
 
             @pl.loop(0, 3)
@@ -192,10 +231,11 @@
             send_parts(jnp.where(which == 0, me, jnp.where(which == 1, other_mid, near_end)))
 
         @pl.loop(0, terms)
-        def _(term):
+        def _(step):
+            term = term_of(step)
             arrived(far_end, term)
 
-            @pl.when(term >= moved)
+            @pl.when(step < terms - moved)
             def _():
                 relay_copy(2, far_end, term, near_end).start()
 
@@ -238,7 +278,7 @@
 
             @pl.loop(moved, terms)
             def _(term):
-                @pl.when(rank > 0)
+                @pl.when((rank > 1) | ((rank == 1) & (term >= moved + early)))
                 def _():
                     arrived(owner, term)
 
@@ -278,13 +318,20 @@
     @pl.when(is_mid)
     def _():
         @pl.loop(0, terms)
-        def _(term):
-            own_copy(0, term, other_mid).wait_send()
+        def _(step):
+            term = term_of(step)
             relay_copy(1, near_end, term, other_mid).wait_send()
 
-            @pl.when(term >= moved)
+            @pl.when(step >= early)
+            def _():
+                own_copy(0, term, other_mid).wait_send()
+
+            @pl.when((step >= early) & (step < terms - moved))
             def _():
                 own_copy(1, term, near_end).wait_send()
+
+            @pl.when(step < terms - moved)
+            def _():
                 relay_copy(0, other_mid, term, near_end).wait_send()
                 relay_copy(2, far_end, term, near_end).wait_send()
 
@@ -292,26 +339,25 @@
 
     @pl.when(is_end)
     def _():
-        @pl.loop(0, terms)
-        def _(term):
-            own_copy(0, term, near_mid).wait_send()
+        @pl.loop(early, terms)
+        def _(step):
+            own_copy(0, term_of(step), near_mid).wait_send()
 
         @pl.loop(0, moved)
         def _(term):
             end_copy(term).wait_send()
 
 
-def line_apply(sectors, dims, state, right, combined):
+def line_apply(sectors, moved, early, dims, state, right, below, above, combined):
     terms, width, cols = right.shape
     rows = state.shape[0]
-    moved = max(1, (terms * 3) // 16)
     tall = combined.shape[1]
     dma = pltpu.SemaphoreType.DMA
     any_space = pl.BlockSpec(memory_space=pl.ANY)
     return pl.pallas_call(
-        functools.partial(line_kernel, sectors, moved),
+        functools.partial(line_kernel, sectors, moved, early),
         out_shape=jax.ShapeDtypeStruct((rows, width), F32),
-        in_specs=[pl.BlockSpec(memory_space=pltpu.SMEM), any_space, any_space, any_space],
+        in_specs=[pl.BlockSpec(memory_space=pltpu.SMEM)] + [any_space] * 5,
         out_specs=pl.BlockSpec(memory_space=pltpu.VMEM),
         scratch_shapes=[
             pltpu.VMEM((4, rows, width), BF16),
@@ -327,7 +373,7 @@
             pltpu.VMEM((4, 4, rows, cols), BF16),
             pltpu.VMEM((4, rows, cols), BF16),
             pltpu.VMEM((4, rows, cols), BF16),
-            dma((3,)), dma((4,)), dma((4,)),
+            dma((5,)), dma((4,)), dma((4,)),
             dma((2, terms)), dma((3, terms)), dma((4, terms)),
             dma((moved,)), dma((moved,)),
             dma((4, 4)), dma((4, 4)), dma((4,)), dma((4,)), dma((2,)),
@@ -335,7 +381,7 @@
         compiler_params=pltpu.CompilerParams(
             has_side_effects=True, vmem_limit_bytes=56 * 2**20
         ),
-    )(dims, state, right, combined)
+    )(dims, state, right, below, above, combined)
 
 
 def passed_along(value, axis, steps):
@@ -372,11 +418,17 @@
     sector = lax.axis_index("sec")
     live_dim = sector_dims[0]
     cells = channel_term * slots + channel_out - sector + 2
+    in_line = lax.axis_size("pan") == 4 and right_blocks.shape[3] % 128 == 0
+    if in_line:
+        moved, early = max(1, terms * 3 // 16), max(1, terms // 4)
+        lead = right_blocks[0, moved:moved + early]
+        below = passed_along(lead, "pan", 1)
+        above = passed_along(lead, "pan", -1)
     combined = combine(cells, coupling.astype(F32), left_blocks, terms * slots)
-    if lax.axis_size("pan") == 4 and right_blocks.shape[3] % 128 == 0:
+    if in_line:
         collected = line_apply(
-            lax.axis_size("sec"), sector_dims, wave_state[0], right_blocks[0],
-            combined.reshape(terms, slots * rows, width),
+            lax.axis_size("sec"), moved, early, sector_dims, wave_state[0], right_blocks[0],
+            below, above, combined.reshape(terms, slots * rows, width),
         )
     else:
         collected = gathered_apply(

time: 153 us -> 150 us (0.980)
  Pallas kernels: 149 us -> 138 us
  starting transfers between devices: 0 us -> 4.81 us
  local copies, waits for them, and re-layouts: 0 us -> 1.88 us
    pallas_call x1, Pallas kernels: 138 us -> 127 us  [line_apply(): pl.pallas_call(functools.partial(line_kernel, sectors, moved, early), out...]
    ppermute x0 -> x2, starting transfers between devices: none -> 4.81 us  [passed_along(): lax.ppermute(value, axis, [(source, source + steps) for source in range(f...]
  transfers between devices with their start and end apart: 0 -> 2, of which waited for: 0 -> 1; matrix products, arithmetic and copies ran while one was open for 0% -> 1% of each run, Pallas kernels for 0% -> 8%
where the time goes in v2:
time: 150 us; the launch traced here: 149 us
  Pallas kernels  138 us (92%)
  starting transfers between devices  4.81 us (3%)
  other arithmetic  3.1 us (2%)
  local copies, waits for them, and re-layouts  1.88 us (1%)
    pallas_call x1, Pallas kernels, line_apply(): pl.pallas_call(functools.partial(line_kernel, sectors, moved, early), out...  127 us
    pallas_call x1, Pallas kernels, combine(): pl.pallas_call(combine_kernel, grid=(rows // step,), in_specs=[pl.BlockSp...  11.4 us
    ppermute x2, starting transfers between devices, passed_along(): lax.ppermute(value, axis, [(source, source + steps) for source in range(f...  4.81 us
  transfers between devices with their start and end apart: 2, of which 1 were waited for; matrix products, arithmetic and copies ran while one was open for 1% of the time, Pallas kernels for 8%

profile of v2, /device:TPU:4, one launch (start us, length us, event | category | flops | bytes accessed | tf_op | source)
XLA Modules:
  0.0 149.5 jit_solution(1807782412559188945)
XLA Ops:
  0.0 1.1 slice_bitcast_fusion
  1.1 3.5 %collective-permute-start = (bf16[4,512,128]{2,1,0:T(8,128)(2,1)S(1)}, bf16[4,512,128]{2,1,0:T(8,128)(2,1)S(1)}, u32[]{:S(2)}, u32[]{:S(2)}) collective-permute-start(bf16[4,512,128]{2,1,0:T(8,128)(2,1)S(1)} %slice_bitcast_fusion), channel_id=1, source_target_pairs={{0,1},{1,2},{2,3},{4,5},{5,6},{6,7},{8,9},{9,10},{10,11},{12,13},{... | collective-permute-start | bytes 1572872 | tf_op jit(solution)/shard_map/ppermute | solution.py:390
  4.6 1.3 collective-permute-start.1
  6.6 0.7 convert_element_type.3.coef_ref
  7.2 0.7 subtract_add_fusion.cell_ref
  7.9 11.4 %shard_map.73 = bf16[80,128,512]{2,1,0:T(8,128)(2,1)} custom-call(s32[72]{0:T(128)S(1)} %subtract_add_fusion.cell_ref, f32[72]{0:T(128)S(1)} %convert_element_type.3.coef_ref, bf16[72,128,512]{2,1,0:T(8,128)(2,1)} %left_ref.1), custom_call_target="tpu_custom_call" | custom-call | flops 9437184 | bytes 99614720 | tf_op jit(solution)/shard_map/pallas_call | solution.py:31
  19.3 0.0 collective-permute-done.below_ref
  19.4 0.0 copy-start
  19.4 0.5 collective-permute-done.1.above_ref
  19.9 0.0 copy-start.1
  19.9 0.3 copy-done
  20.2 0.5 copy-done.1
  20.7 127.0 %shard_map.74 = f32[128,512]{1,0:T(8,128)} custom-call(s32[1]{0:T(128)} %copy.8.dims_ref, bf16[128,512]{1,0:T(8,128)(2,1)} %bitcast.12, bf16[16,512,128]{2,1,0:T(8,128)(2,1)} %bitcast.11, bf16[4,512,128]{2,1,0:T(8,128)(2,1)} %copy-done, bf16[4,512,128]{2,1,0:T(8,128)(2,1)} %copy-done.1, bf16[16,640,512]{2,1,0:T(8,128)(2,1)} %bitcast.10), custom_call_target="tpu_custom_call" | custom-call | tf_op jit(solution)/shard_map/pallas_call | solution.py:357
  147.7 1.8 %select_bitcast_fusion = f32[1,128,512]{2,1,0:T(8,128)} fusion(f32[128,512]{1,0:T(8,128)} %shard_map.74, pred[512]{0:T(512)(128)(4,1)S(1)} %iota_compare_fusion, pred[128]{0:T(512)(128)(4,1)S(1)} %add_compare_fusion), kind=kLoop, calls=%fused_computation.1 | loop fusion | flops 131072 | bytes 524928 | tf_op jit(solution)/shard_map/broadcast_in_dim | solution.py:440
  (2 shorter events, 0.0 us)
Async XLA Ops:
  1.1 18.3 %collective-permute-start = (bf16[4,512,128]{2,1,0:T(8,128)(2,1)S(1)}, bf16[4,512,128]{2,1,0:T(8,128)(2,1)S(1)}, u32[]{:S(2)}, u32[]{:S(2)}) collective-permute-start(bf16[4,512,128]{2,1,0:T(8,128)(2,1)S(1)} %slice_bitcast_fusion), channel_id=1, source_target_pairs={{0,1},{1,2},{2,3},{4,5},{5,6},{6,7},{8,9},{9,10},{10,11},{12,13},{... | collective-permute-start | bytes 1572872 | tf_op jit(solution)/shard_map/ppermute | solution.py:390
  4.6 15.3 %collective-permute-start.1 = (bf16[4,512,128]{2,1,0:T(8,128)(2,1)S(1)}, bf16[4,512,128]{2,1,0:T(8,128)(2,1)S(1)}, u32[]{:S(2)}, u32[]{:S(2)}) collective-permute-start(bf16[4,512,128]{2,1,0:T(8,128)(2,1)S(1)} %slice_bitcast_fusion), channel_id=1, source_target_pairs={{1,0},{2,1},{3,2},{5,4},{6,5},{7,6},{9,8},{10,9},{11,10},{13,12},{... | collective-permute-start | bytes 1572872 | tf_op jit(solution)/shard_map/ppermute | solution.py:390
  19.4 0.8 copy-start
  19.9 0.8 copy-start.1

commit v3 on v1

--- a/solution.py
+++ b/solution.py
@@ -43,8 +43,71 @@
     )(cells, coefs, left_blocks)
 
 
+def order_kernel(slots, term_ref, out_ids_ref, coef_ref, table_ref, sorted_ref, spots):
+    channels = term_ref.shape[0]
+    cells = spots.shape[0]
+    last_at, filled_at = 2 * channels, 2 * channels + cells
+    sector = lax.axis_index("sec")
+
+    def cell_of(channel):
+        return term_ref[channel] * slots + out_ids_ref[channel] - sector + 2
+
+    @pl.loop(0, cells)
+    def _(cell):
+        spots[cell] = 0
+
+    @pl.loop(0, channels)
+    def _(channel):
+        spots[cell_of(channel)] += 1
+
+    def lay_out(cell, start):
+        count = spots[cell]
+        spots[cell] = start
+        table_ref[last_at + cell] = jnp.maximum(start + count - 1, 0)
+        table_ref[filled_at + cell] = jnp.minimum(count, 1)
+        return start + count
+
+    lax.fori_loop(0, cells, lay_out, 0)
+
+    @pl.loop(0, channels)
+    def _(channel):
+        table_ref[channels + channel] = 1
+
+    @pl.loop(0, cells)
+    def _(cell):
+        table_ref[channels + jnp.minimum(spots[cell], channels - 1)] = jnp.where(
+            table_ref[filled_at + cell] > 0,
+            0,
+            table_ref[channels + jnp.minimum(spots[cell], channels - 1)],
+        )
+
+    @pl.loop(0, channels)
+    def _(channel):
+        cell = cell_of(channel)
+        spot = spots[cell]
+        spots[cell] = spot + 1
+        table_ref[spot] = channel
+        sorted_ref[spot] = coef_ref[channel]
+
+
+def order_channels(slots, cells, channel_term, channel_out, coefs):
+    channels = coefs.shape[0]
+    smem = pl.BlockSpec(memory_space=pltpu.SMEM)
+    return pl.pallas_call(
+        functools.partial(order_kernel, slots),
+        out_shape=(
+            jax.ShapeDtypeStruct((2 * channels + 2 * cells,), jnp.int32),
+            jax.ShapeDtypeStruct((channels,), F32),
+        ),
+        in_specs=[smem] * 3,
+        out_specs=(smem, smem),
+        scratch_shapes=[pltpu.SMEM((cells,), jnp.int32)],
+    )(channel_term, channel_out, coefs)
+
+
 def line_kernel(
-    sectors, moved, dims_ref, state_ref, right_ref, comb_ref, out_ref,
+    sectors, moved, dims_ref, table_ref, coef_ref, state_ref, right_ref, left_ref, out_ref,
+    left_all, running, summed,
     state_all, masked, gathered, comb, comb_end, acc, acc_end,
     stage, landed, stage_end, landed_end, back, back_landed,
     local_sems, state_send, state_recv, own_send, relay_send, right_recv,
@@ -52,6 +115,7 @@
 ):
     terms, width, cols = right_ref.shape
     rows = state_ref.shape[0]
+    slots = comb.shape[1] // rows
     me = lax.axis_index("pan")
     sector = lax.axis_index("sec")
     is_mid = (me == 1) | (me == 2)
@@ -86,7 +150,7 @@
         return remote(block, block, relay_send.at[way, term], right_recv.at[owner, term], where)
 
     def end_copy(term):
-        return remote(comb_ref.at[term], comb_end.at[term], end_send.at[term], end_recv.at[term], near_mid)
+        return remote(comb.at[term], comb_end.at[term], end_send.at[term], end_recv.at[term], near_mid)
 
     def arrived(owner, term):
         block = gathered.at[owner, term]
@@ -131,23 +195,46 @@
         def _(term):
             own_copy(0, term, near_mid).start()
 
-        @pl.loop(0, moved)
-        def _(term):
-            end_copy(term).start()
-
     copies = [
         pltpu.make_async_copy(state_ref, state_all.at[me], local_sems.at[0]),
         pltpu.make_async_copy(right_ref, gathered.at[me], local_sems.at[1]),
-        pltpu.make_async_copy(comb_ref, comb, local_sems.at[2]),
+        pltpu.make_async_copy(left_ref, left_all, local_sems.at[2]),
     ]
     for copy in copies:
         copy.start()
     acc[...] = jnp.zeros_like(acc)
     acc_end[...] = jnp.zeros_like(acc_end)
+    running[...] = jnp.zeros_like(running)
     for copy in copies:
         copy.wait()
+
+    channels = left_all.shape[0]
+    cells = terms * slots
+
+    @pl.loop(0, channels)
+    def _(step):
+        kept = table_ref[channels + step].astype(F32)
+        total = running[...] * kept + left_all[table_ref[step]].astype(F32) * coef_ref[step]
+        running[...] = total
+        summed[step] = total.astype(BF16)
+
+    @pl.loop(0, terms)
+    def _(term):
+        for slot in range(slots):
+            cell = term * slots + slot
+            filled = table_ref[2 * channels + cells + cell].astype(F32)
+            value = summed[table_ref[2 * channels + cell]].astype(F32) * filled
+            comb[term, slot * rows:(slot + 1) * rows, :] = value.astype(BF16)
+
     for shift in (1, 2, 3):
         state_wait(lax.rem(me + shift, 4))
+
+    @pl.when(is_end)
+    def _():
+        @pl.loop(0, moved)
+        def _(term):
+            end_copy(term).start()
+
     live = dims_ref[0]
     inside_col = lax.broadcasted_iota(jnp.int32, (rows, width), 1) < live
     for owner in range(4):
@@ -205,7 +292,7 @@
 
         @pl.loop(0, moved)
         def _(term):
-            remote(comb_ref.at[term], comb_end.at[term], end_send.at[term], end_recv.at[term], me).wait_recv()
+            remote(comb.at[term], comb_end.at[term], end_send.at[term], end_recv.at[term], me).wait_recv()
 
             @pl.loop(0, 4)
             def _(owner):
@@ -301,19 +388,22 @@
             end_copy(term).wait_send()
 
 
-def line_apply(sectors, dims, state, right, combined):
+def line_apply(sectors, slots, dims, table, coefs, state, right, left):
     terms, width, cols = right.shape
     rows = state.shape[0]
     moved = max(1, (terms * 3) // 16)
-    tall = combined.shape[1]
+    tall = slots * rows
     dma = pltpu.SemaphoreType.DMA
     any_space = pl.BlockSpec(memory_space=pl.ANY)
     return pl.pallas_call(
         functools.partial(line_kernel, sectors, moved),
         out_shape=jax.ShapeDtypeStruct((rows, width), F32),
-        in_specs=[pl.BlockSpec(memory_space=pltpu.SMEM), any_space, any_space, any_space],
+        in_specs=[pl.BlockSpec(memory_space=pltpu.SMEM)] * 3 + [any_space] * 3,
         out_specs=pl.BlockSpec(memory_space=pltpu.VMEM),
         scratch_shapes=[
+            pltpu.VMEM(left.shape, BF16),
+            pltpu.VMEM((rows, width), F32),
+            pltpu.VMEM(left.shape, BF16),
             pltpu.VMEM((4, rows, width), BF16),
             pltpu.VMEM((width, width), BF16),
             pltpu.VMEM((4, terms, width, cols), BF16),
@@ -335,7 +425,7 @@
         compiler_params=pltpu.CompilerParams(
             has_side_effects=True, vmem_limit_bytes=56 * 2**20
         ),
-    )(dims, state, right, combined)
+    )(dims, table, coefs, state, right, left)
 
 
 def passed_along(value, axis, steps):
@@ -372,13 +462,15 @@
     sector = lax.axis_index("sec")
     live_dim = sector_dims[0]
     cells = channel_term * slots + channel_out - sector + 2
-    combined = combine(cells, coupling.astype(F32), left_blocks, terms * slots)
+    coefs = coupling.astype(F32)
     if lax.axis_size("pan") == 4 and right_blocks.shape[3] % 128 == 0:
+        table, ordered = order_channels(slots, terms * slots, channel_term, channel_out, coefs)
         collected = line_apply(
-            lax.axis_size("sec"), sector_dims, wave_state[0], right_blocks[0],
-            combined.reshape(terms, slots * rows, width),
+            lax.axis_size("sec"), slots, sector_dims, table, ordered,
+            wave_state[0], right_blocks[0], left_blocks,
         )
     else:
+        combined = combine(cells, coefs, left_blocks, terms * slots)
         collected = gathered_apply(
             sector, live_dim, wave_state[0], right_blocks[0], combined, rows, slots
         )

time: 153 us -> 147 us (0.961)
  Pallas kernels: 149 us -> 144 us
    pallas_call x1, Pallas kernels: 11.5 us -> 5.46 us  [order_channels(): pl.pallas_call(functools.partial(order_kernel, slots), out_shape=(jax.Sha...]
where the time goes in v3:
time: 147 us
  Pallas kernels  144 us (98%)
  other arithmetic  2.92 us (2%)
    pallas_call x1, Pallas kernels, line_apply(): pl.pallas_call(functools.partial(line_kernel, sectors, moved), out_shape=...  138 us
    pallas_call x1, Pallas kernels, order_channels(): pl.pallas_call(functools.partial(order_kernel, slots), out_shape=(jax.Sha...  5.46 us

profile of v3, /device:TPU:4, one launch (start us, length us, event | category | flops | bytes accessed | tf_op | source)
XLA Modules:
  0.0 147.3 jit_solution(12505389195447245324)
XLA Ops:
  0.7 1.2 convert_element_type.3.coef_ref
  1.8 5.5 %shard_map.73 = (s32[304]{0:T(512)}, f32[72]{0:T(128)}) custom-call(s32[72]{0:T(128)} %term_ref.1, s32[72]{0:T(128)} %out_ids_ref.1, f32[72]{0:T(128)} %convert_element_type.3.coef_ref), custom_call_target="tpu_custom_call" | custom-call | tf_op jit(solution)/shard_map/pallas_call | solution.py:96
  7.3 138.2 %shard_map.74 = f32[128,512]{1,0:T(8,128)} custom-call(s32[1]{0:T(128)} %copy.8.dims_ref, s32[304]{0:T(512)} %get-tuple-element.7.table_ref, f32[72]{0:T(128)} %get-tuple-element.8.coef_ref, bf16[128,512]{1,0:T(8,128)(2,1)} %bitcast.8, bf16[16,512,128]{2,1,0:T(8,128)(2,1)} %bitcast.7, bf16[72,128,512]{2,1,0:T(8,128)(2,1)} %left_ref.1), custom_call_target="tpu_custom_call" | custom-call | tf_op jit(solution)/shard_map/pallas_call | solution.py:398
  145.6 1.8 %select_bitcast_fusion = f32[1,128,512]{2,1,0:T(8,128)} fusion(f32[128,512]{1,0:T(8,128)} %shard_map.74, pred[512]{0:T(512)(128)(4,1)S(1)} %iota_compare_fusion, pred[128]{0:T(512)(128)(4,1)S(1)} %add_compare_fusion), kind=kLoop, calls=%fused_computation | loop fusion | flops 131072 | bytes 524928 | tf_op jit(solution)/shard_map/broadcast_in_dim | solution.py:480
  (2 shorter events, 0.0 us)

commit v4 on v3

--- a/solution.py
+++ b/solution.py
@@ -152,6 +152,9 @@
     def end_copy(term):
         return remote(comb.at[term], comb_end.at[term], end_send.at[term], end_recv.at[term], near_mid)
 
+    def end_copy_arrived(term):
+        remote(comb.at[term], comb_end.at[term], end_send.at[term], end_recv.at[term], me).wait_recv()
+
     def arrived(owner, term):
         block = gathered.at[owner, term]
         remote(block, block, relay_send.at[0, term], right_recv.at[owner, term], me).wait_recv()
@@ -189,9 +192,11 @@
             def _():
                 own_copy(1, term, near_end).start()
 
+    ahead = terms * 3 // 8
+
     @pl.when(is_end)
     def _():
-        @pl.loop(0, terms)
+        @pl.loop(0, ahead)
         def _(term):
             own_copy(0, term, near_mid).start()
 
@@ -231,9 +236,19 @@
 
     @pl.when(is_end)
     def _():
-        @pl.loop(0, moved)
-        def _(term):
-            end_copy(term).start()
+        for turn in range(moved):
+            left = terms - ahead
+            first = ahead + left * turn // moved
+
+            @pl.when(turn < moved - 1)
+            def _():
+                end_copy(turn).start()
+
+            @pl.loop(first, ahead + left * (turn + 1) // moved)
+            def _(term):
+                own_copy(0, term, near_mid).start()
+
+        end_copy(moved - 1).start()
 
     live = dims_ref[0]
     inside_col = lax.broadcasted_iota(jnp.int32, (rows, width), 1) < live
@@ -256,47 +271,65 @@
                 stage[index, owner] = acc[owner, slot * rows:(slot + 1) * rows, :].astype(BF16)
                 part_copy(index, owner).start()
 
+    end_lag, far_lag, extra_lag = terms * 3 // 8, terms * 11 // 16, terms * 11 // 8
+
+    def extra(term):
+        end_copy_arrived(term)
+
+        @pl.loop(0, 4)
+        def _(owner):
+            multiply(owner, term, comb_end, acc_end)
+
     @pl.when(is_mid)
     def _():
-        @pl.loop(0, terms)
-        def _(term):
-            arrived(other_mid, term)
-
-            @pl.when(term >= moved)
-            def _():
-                relay_copy(0, other_mid, term, near_end).start()
-
-            arrived(near_end, term)
-            relay_copy(1, near_end, term, other_mid).start()
-
-            @pl.loop(0, 3)
-            def _(which):
-                owner = jnp.where(which == 0, me, jnp.where(which == 1, other_mid, near_end))
-                multiply(owner, term, comb, acc)
-
-        @pl.loop(0, 3)
-        def _(which):
-            send_parts(jnp.where(which == 0, me, jnp.where(which == 1, other_mid, near_end)))
-
-        @pl.loop(0, terms)
-        def _(term):
-            arrived(far_end, term)
-
-            @pl.when(term >= moved)
-            def _():
-                relay_copy(2, far_end, term, near_end).start()
-
-            multiply(far_end, term, comb, acc)
-
-        send_parts(far_end)
-
-        @pl.loop(0, moved)
-        def _(term):
-            remote(comb.at[term], comb_end.at[term], end_send.at[term], end_recv.at[term], me).wait_recv()
-
-            @pl.loop(0, 4)
-            def _(owner):
-                multiply(owner, term, comb_end, acc_end)
+        @pl.loop(0, terms + far_lag)
+        def _(tick):
+            near, far, late = tick - end_lag, tick - far_lag, tick - extra_lag
+
+            @pl.when(tick < terms)
+            def _():
+                arrived(other_mid, tick)
+
+                @pl.when(tick >= moved)
+                def _():
+                    relay_copy(0, other_mid, tick, near_end).start()
+
+            @pl.when((near >= 0) & (near < terms))
+            def _():
+                arrived(near_end, near)
+                relay_copy(1, near_end, near, other_mid).start()
+
+            @pl.when(far >= 0)
+            def _():
+                arrived(far_end, far)
+
+                @pl.when(far >= moved)
+                def _():
+                    relay_copy(2, far_end, far, near_end).start()
+
+            @pl.when(tick < terms)
+            def _():
+                @pl.loop(0, 2)
+                def _(which):
+                    multiply(jnp.where(which == 0, me, other_mid), tick, comb, acc)
+
+            @pl.when((near >= 0) & (near < terms))
+            def _():
+                multiply(near_end, near, comb, acc)
+
+            @pl.when(far >= 0)
+            def _():
+                multiply(far_end, far, comb, acc)
+
+            @pl.when((late >= 0) & (late < moved - 1))
+            def _():
+                extra(late)
+
+        @pl.loop(0, 4)
+        def _(owner):
+            send_parts(owner)
+
+        extra(moved - 1)
 
         for index in range(4):
             slot = OFFSETS[index] + 2
@@ -391,7 +424,7 @@
 def line_apply(sectors, slots, dims, table, coefs, state, right, left):
     terms, width, cols = right.shape
     rows = state.shape[0]
-    moved = max(1, (terms * 3) // 16)
+    moved = max(1, terms // 4)
     tall = slots * rows
     dma = pltpu.SemaphoreType.DMA
     any_space = pl.BlockSpec(memory_space=pl.ANY)

time: 147 us -> 154 us (1.048)
  Pallas kernels: 144 us -> 150 us
    pallas_call x1, Pallas kernels: 138 us -> 145 us  [line_apply(): pl.pallas_call(functools.partial(line_kernel, sectors, moved), out_shape=...]
where the time goes in v4:
time: 154 us
  Pallas kernels  150 us (97%)
  other arithmetic  2.92 us (2%)
    pallas_call x1, Pallas kernels, line_apply(): pl.pallas_call(functools.partial(line_kernel, sectors, moved), out_shape=...  145 us
    pallas_call x1, Pallas kernels, order_channels(): pl.pallas_call(functools.partial(order_kernel, slots), out_shape=(jax.Sha...  5.46 us

profile of v4, /device:TPU:4, one launch (start us, length us, event | category | flops | bytes accessed | tf_op | source)
XLA Modules:
  0.0 154.0 jit_solution(4923805414880035671)
XLA Ops:
  0.7 1.2 convert_element_type.3.coef_ref
  1.8 5.5 %shard_map.73 = (s32[304]{0:T(512)}, f32[72]{0:T(128)}) custom-call(s32[72]{0:T(128)} %term_ref.1, s32[72]{0:T(128)} %out_ids_ref.1, f32[72]{0:T(128)} %convert_element_type.3.coef_ref), custom_call_target="tpu_custom_call" | custom-call | tf_op jit(solution)/shard_map/pallas_call | solution.py:96
  7.3 145.0 %shard_map.74 = f32[128,512]{1,0:T(8,128)} custom-call(s32[1]{0:T(128)} %copy.8.dims_ref, s32[304]{0:T(512)} %get-tuple-element.7.table_ref, f32[72]{0:T(128)} %get-tuple-element.8.coef_ref, bf16[128,512]{1,0:T(8,128)(2,1)} %bitcast.8, bf16[16,512,128]{2,1,0:T(8,128)(2,1)} %bitcast.7, bf16[72,128,512]{2,1,0:T(8,128)(2,1)} %left_ref.1), custom_call_target="tpu_custom_call" | custom-call | tf_op jit(solution)/shard_map/pallas_call | solution.py:431
  152.3 1.8 %select_bitcast_fusion = f32[1,128,512]{2,1,0:T(8,128)} fusion(f32[128,512]{1,0:T(8,128)} %shard_map.74, pred[512]{0:T(512)(128)(4,1)S(1)} %iota_compare_fusion, pred[128]{0:T(512)(128)(4,1)S(1)} %add_compare_fusion), kind=kLoop, calls=%fused_computation | loop fusion | flops 131072 | bytes 524928 | tf_op jit(solution)/shard_map/broadcast_in_dim | solution.py:513
  (2 shorter events, 0.0 us)

commit v5 on v3

--- a/solution.py
+++ b/solution.py
@@ -52,36 +52,28 @@
     def cell_of(channel):
         return term_ref[channel] * slots + out_ids_ref[channel] - sector + 2
 
-    @pl.loop(0, cells)
+    @pl.loop(0, cells, unroll=8)
     def _(cell):
         spots[cell] = 0
 
-    @pl.loop(0, channels)
+    @pl.loop(0, channels, unroll=4)
     def _(channel):
         spots[cell_of(channel)] += 1
+        table_ref[channels + channel] = 1
 
     def lay_out(cell, start):
         count = spots[cell]
         spots[cell] = start
         table_ref[last_at + cell] = jnp.maximum(start + count - 1, 0)
-        table_ref[filled_at + cell] = jnp.minimum(count, 1)
+        filled = jnp.minimum(count, 1)
+        table_ref[filled_at + cell] = filled
+        first = channels + jnp.minimum(start, channels - 1)
+        table_ref[first] = jnp.where(count > 0, 0, table_ref[first])
         return start + count
 
-    lax.fori_loop(0, cells, lay_out, 0)
-
-    @pl.loop(0, channels)
-    def _(channel):
-        table_ref[channels + channel] = 1
-
-    @pl.loop(0, cells)
-    def _(cell):
-        table_ref[channels + jnp.minimum(spots[cell], channels - 1)] = jnp.where(
-            table_ref[filled_at + cell] > 0,
-            0,
-            table_ref[channels + jnp.minimum(spots[cell], channels - 1)],
-        )
-
-    @pl.loop(0, channels)
+    lax.fori_loop(0, cells, lay_out, 0, unroll=4)
+
+    @pl.loop(0, channels, unroll=4)
     def _(channel):
         cell = cell_of(channel)
         spot = spots[cell]
@@ -391,7 +383,7 @@
 def line_apply(sectors, slots, dims, table, coefs, state, right, left):
     terms, width, cols = right.shape
     rows = state.shape[0]
-    moved = max(1, (terms * 3) // 16)
+    moved = max(1, terms // 4)
     tall = slots * rows
     dma = pltpu.SemaphoreType.DMA
     any_space = pl.BlockSpec(memory_space=pl.ANY)

time: 147 us -> 148 us (level)
    pallas_call x1, Pallas kernels: 138 us -> 141 us  [line_apply(): pl.pallas_call(functools.partial(line_kernel, sectors, moved), out_shape=...]
    pallas_call x1, Pallas kernels: 5.46 us -> 2.86 us  [order_channels(): pl.pallas_call(functools.partial(order_kernel, slots), out_shape=(jax.Sha...]
where the time goes in v5:
time: 148 us
  Pallas kernels  144 us (97%)
  other arithmetic  2.92 us (2%)
    pallas_call x1, Pallas kernels, line_apply(): pl.pallas_call(functools.partial(line_kernel, sectors, moved), out_shape=...  141 us

profile of v5, /device:TPU:4, one launch (start us, length us, event | category | flops | bytes accessed | tf_op | source)
XLA Modules:
  0.0 147.8 jit_solution(3642623875544986229)
XLA Ops:
  0.7 1.2 convert_element_type.3.coef_ref
  1.8 2.9 %shard_map.73 = (s32[304]{0:T(512)}, f32[72]{0:T(128)}) custom-call(s32[72]{0:T(128)} %term_ref.1, s32[72]{0:T(128)} %out_ids_ref.1, f32[72]{0:T(128)} %convert_element_type.3.coef_ref), custom_call_target="tpu_custom_call" | custom-call | tf_op jit(solution)/shard_map/pallas_call | solution.py:88
  4.7 141.4 %shard_map.74 = f32[128,512]{1,0:T(8,128)} custom-call(s32[1]{0:T(128)} %copy.8.dims_ref, s32[304]{0:T(512)} %get-tuple-element.7.table_ref, f32[72]{0:T(128)} %get-tuple-element.8.coef_ref, bf16[128,512]{1,0:T(8,128)(2,1)} %bitcast.8, bf16[16,512,128]{2,1,0:T(8,128)(2,1)} %bitcast.7, bf16[72,128,512]{2,1,0:T(8,128)(2,1)} %left_ref.1), custom_call_target="tpu_custom_call" | custom-call | tf_op jit(solution)/shard_map/pallas_call | solution.py:390
  146.1 1.8 %select_bitcast_fusion = f32[1,128,512]{2,1,0:T(8,128)} fusion(f32[128,512]{1,0:T(8,128)} %shard_map.74, pred[512]{0:T(512)(128)(4,1)S(1)} %iota_compare_fusion, pred[128]{0:T(512)(128)(4,1)S(1)} %add_compare_fusion), kind=kLoop, calls=%fused_computation | loop fusion | flops 131072 | bytes 524928 | tf_op jit(solution)/shard_map/broadcast_in_dim | solution.py:472
  (2 shorter events, 0.0 us)
